TPU v7x, 256 devices: a whole 4x4x8 slice. The times are simulated.
256 devices in a mesh: dp: 2 (over core), section: 8 (over z), mp: 16 (over y, x).
Axes of the slice: x: 4, y: 4, z: 8, core: 2. Of those that a mesh axis runs over, the one named last changes fastest.
Arguments:
- inputs: bfloat16 [192, 512], P(('dp', 'mp')), may hold values from -6 to 6
- tangents: bfloat16 [192, 32, 512], P(('dp', 'mp')), may hold values from -6 to 6
- targets: bfloat16 [192, 1024], P(('dp', 'mp')), may hold values from -24 to 24
- target_jac: bfloat16 [192, 32, 1024], P(('dp', 'mp')), may hold values from -24 to 24
- rank_mask: int32 [192, 32], P(('dp', 'mp')), may hold values from 0 to 1, as said below
- batch_order: int32 [32, 6], P(('dp', 'mp')), may hold values from 0 to 5, each once within a row
- encoder: bfloat16 [512, 2048], replicated, may hold values from -0.25 to 0.25
- layers: bfloat16 [8, 2048, 2048], P('section', 'mp'), may hold values from -0.125 to 0.125
- head_weight: bfloat16 [2048, 1024], replicated, may hold values from -0.125 to 0.125
Outputs:
- grad_layers: float32 [8, 2048, 2048], P('section', ('dp', 'mp'))
- grad_head: float32 [2048, 1024], P(('dp', 'mp'), 'section')
- loss_value: float32 [], replicated
Inputs may be any that keep to these rules, and one draw needn't show every extreme that they name: `rank_mask`: each sample's ones are its first 1 to 32 directions. `batch_order`: each row is an ordering of 0 .. 5.
All inputs are finite; a program needn't handle non-finite values.
Results may differ from a plain program's by a relative error of at most 0.035.
Values may be sent and summed in bfloat16 or wider, within the bound.
A program may use at most 128 MiB of HBM per device.

v0:
```python
import jax
import jax.numpy as jnp
from jax import lax
from jax.sharding import PartitionSpec as P

MB = 6


def from_behind(value, axis, steps):
    count = lax.axis_size(axis)
    initial, last = (max(0, -steps), min(count, count - steps))
    return lax.ppermute(value, axis, [(source, source + steps) for source in range(initial, last)])


def in_blocks(array, dim, count):
    before, after = (array.shape[:dim], array.shape[dim + 1 :])
    return jnp.moveaxis(array.reshape(*before, count, -1, *after), dim, 0)


def sent_and_summed(array, axis, dim):
    parts = in_blocks(array, dim, lax.axis_size(axis))
    arrived = lax.all_to_all(parts, axis, split_axis=0, concat_axis=0, tiled=True)
    return arrived.astype(jnp.float32).sum(axis=0)


def from_everyone(array, axis):
    count = lax.axis_size(axis)
    return lax.all_to_all(
        jnp.broadcast_to(array[None], (count, *array.shape)), axis, 0, 0, tiled=True
    )


def over_copies(array, axis):
    return from_everyone(array, axis).sum(axis=0)


def forward_layer(row_block, weight):
    model_width = weight.shape[1]
    pre_act = jnp.dot(
        row_block.reshape(-1, model_width), weight, preferred_element_type=jnp.float32
    ).reshape(row_block.shape)
    tanh_p = jnp.tanh(pre_act[:, 0])
    slope_vals = 1.0 - tanh_p * tanh_p
    primal = row_block[:, 0].astype(jnp.float32) + tanh_p
    tangent = row_block[:, 1:].astype(jnp.float32) + slope_vals[:, None, :] * pre_act[:, 1:]
    return (jnp.concatenate([primal[:, None], tangent], axis=1).astype(jnp.bfloat16), pre_act)


def backward_layer(pre_act, grad_rows, weight):
    model_width = weight.shape[1]
    upstream = grad_rows.astype(jnp.float32)
    tanh_p = jnp.tanh(pre_act[:, 0])
    slope_vals = 1.0 - tanh_p * tanh_p
    tangent_part = upstream[:, 1:] * slope_vals[:, None, :]
    slope_grad = jnp.sum(upstream[:, 1:] * pre_act[:, 1:], axis=1)
    primal_part = upstream[:, 0] * slope_vals - 2.0 * slope_grad * tanh_p * slope_vals
    grad_mix = jnp.concatenate([primal_part[:, None], tangent_part], axis=1).astype(jnp.bfloat16)
    back_rows = jnp.dot(
        grad_mix.reshape(-1, model_width), weight.T, preferred_element_type=jnp.float32
    ).reshape(upstream.shape)
    return (grad_mix, (upstream + back_rows).astype(jnp.bfloat16))


def place_slot(store, value, batch_slot, is_valid):
    return lax.dynamic_update_index_in_dim(
        store, jnp.where(is_valid, value, store[batch_slot]), batch_slot, 0
    )


def local(
    inputs, tangents, targets, target_jac, rank_mask, batch_order, encoder, layers, head_weight
):
    samp_dev = inputs.shape[0]
    per_batch = samp_dev // MB
    row_depth = tangents.shape[1] + 1
    in_width = inputs.shape[1]
    model_width = layers.shape[2]
    out_width = head_weight.shape[1]
    sections = lax.axis_size("section")
    section_id = lax.axis_index("section")
    is_first = section_id == 0
    is_last = section_id == sections - 1
    layer_full = lax.all_gather(layers[0], "mp", axis=0, tiled=True)
    sample_order = batch_order[0]
    row_weight = jnp.concatenate(
        [jnp.ones((samp_dev, 1), jnp.float32), rank_mask.astype(jnp.float32)], axis=1
    )
    sample_total = jnp.sum(row_weight, axis=1)
    batch_counts = lax.psum(
        jnp.sum(sample_total[sample_order].reshape(MB, per_batch), axis=1), "mp"
    )

    def picked_of(batch_slot):
        return lax.dynamic_slice_in_dim(sample_order, batch_slot * per_batch, per_batch)

    def lift_batch(batch_slot):
        picked = picked_of(batch_slot)
        rows_in = jnp.concatenate([inputs[picked][:, None, :], tangents[picked]], axis=1)
        lifted = jnp.dot(rows_in.reshape(-1, in_width), encoder, preferred_element_type=jnp.float32)
        return lifted.reshape(per_batch, row_depth, model_width).astype(jnp.bfloat16)

    block_shape = (MB, per_batch, row_depth, model_width)
    pre_shape = (1, 1, 1, 1)

    def forward_tick(step_index, loop_state):
        incoming, store_in, store_pre, store_out = loop_state
        batch_index = step_index - section_id
        is_valid = (batch_index >= 0) & (batch_index < MB)
        batch_slot = jnp.clip(batch_index, 0, MB - 1)
        row_block = lax.cond(is_first, lambda: lift_batch(batch_slot), lambda: incoming)

        def forward_active():
            return forward_layer(row_block, layer_full)

        def forward_resting():
            return (row_block, jnp.zeros(row_block.shape, jnp.float32))

        layer_out, pre_act = lax.cond(is_valid, forward_active, forward_resting)
        store_in = place_slot(store_in, row_block, batch_slot, is_valid)
        store_out = place_slot(store_out, layer_out, batch_slot, is_valid)
        passed = from_behind(layer_out, "section", 1)
        return (passed, store_in, store_pre, store_out)

    start_state = (
        jnp.zeros(block_shape[1:], jnp.bfloat16),
        jnp.zeros(block_shape, jnp.bfloat16),
        jnp.zeros(pre_shape, jnp.float32),
        jnp.zeros(block_shape, jnp.bfloat16),
    )
    _, store_in, store_pre, store_out = lax.fori_loop(
        0, MB + sections - 1, forward_tick, start_state
    )

    def backward_tick(step_index, loop_state):
        incoming, store_mix, store_head, loss_acc = loop_state
        batch_index = step_index - (sections - 1 - section_id)
        is_valid = (batch_index >= 0) & (batch_index < MB)
        batch_slot = jnp.clip(batch_index, 0, MB - 1)
        batch_total = batch_counts[batch_slot]

        def head_part():
            final_rows = store_out[batch_slot]
            outputs = jnp.dot(
                final_rows.reshape(-1, model_width), head_weight, preferred_element_type=jnp.float32
            )
            outputs = outputs.reshape(per_batch, row_depth, out_width)
            picked = picked_of(batch_slot)
            wanted = jnp.concatenate(
                [targets[picked][:, None, :], target_jac[picked]], axis=1
            ).astype(jnp.float32)
            weights_here = row_weight[picked]
            mismatch = outputs - wanted
            misfit = jnp.sum(weights_here[:, :, None] * mismatch * mismatch) / batch_total
            cot_out = (2.0 * weights_here[:, :, None] * mismatch / batch_total).astype(jnp.bfloat16)
            grad_rows = jnp.dot(
                cot_out.reshape(-1, out_width), head_weight.T, preferred_element_type=jnp.float32
            )
            return (
                grad_rows.reshape(per_batch, row_depth, model_width).astype(jnp.bfloat16),
                cot_out,
                misfit,
            )

        def pass_on():
            return (
                incoming,
                jnp.zeros((per_batch, row_depth, out_width), jnp.bfloat16),
                jnp.zeros((), jnp.float32),
            )

        grad_rows, cot_out, misfit = lax.cond(is_last & is_valid, head_part, pass_on)

        def backward_active():
            row_block = store_in[batch_slot]
            pre_act = jnp.dot(
                row_block.reshape(-1, model_width), layer_full, preferred_element_type=jnp.float32
            ).reshape(row_block.shape)
            return backward_layer(pre_act, grad_rows, layer_full)

        def backward_resting():
            return (jnp.zeros(grad_rows.shape, jnp.bfloat16), grad_rows)

        grad_mix, grad_in = lax.cond(is_valid, backward_active, backward_resting)
        store_mix = place_slot(store_mix, grad_mix, batch_slot, is_valid)
        store_head = place_slot(store_head, cot_out, batch_slot, is_valid)
        loss_acc = loss_acc + jnp.where(is_valid, misfit, jnp.zeros((), jnp.float32))
        passed = from_behind(grad_in, "section", -1)
        return (passed, store_mix, store_head, loss_acc)

    back_state = (
        jnp.zeros(block_shape[1:], jnp.bfloat16),
        jnp.zeros(block_shape, jnp.bfloat16),
        jnp.zeros((MB, per_batch, row_depth, out_width), jnp.bfloat16),
        jnp.zeros((), jnp.float32),
    )
    _, store_mix, store_head, loss_acc = lax.fori_loop(
        0, MB + sections - 1, backward_tick, back_state
    )
    shard_rows = model_width // (lax.axis_size("dp") * lax.axis_size("mp"))
    in_flat = store_in.reshape(-1, model_width)
    mix_flat = store_mix.reshape(-1, model_width)
    grad_layers = lax.psum_scatter(
        jnp.dot(in_flat.T, mix_flat, preferred_element_type=jnp.float32).astype(jnp.bfloat16),
        ("dp", "mp"),
        scatter_dimension=0,
        tiled=True,
    ).astype(jnp.float32)[None]
    out_flat = store_out.reshape(-1, model_width)
    head_flat = store_head.reshape(-1, out_width)

    def compute():
        return jnp.dot(out_flat.T, head_flat, preferred_element_type=jnp.float32)

    def skipped():
        return jnp.zeros((shard_rows * lax.axis_size(("dp", "mp")), out_width), jnp.float32)

    summed = sent_and_summed(
        lax.cond(is_last, compute, skipped).astype(jnp.bfloat16), ("dp", "mp"), 0
    )
    section_loss = over_copies(loss_acc, ("dp", "mp"))
    loss_row = jnp.broadcast_to(section_loss, (1, sections))
    grad_head, loss_cols = (
        sent_and_summed(summed.astype(jnp.bfloat16), "section", 1),
        sent_and_summed(loss_row.astype(jnp.bfloat16), "section", 1),
    )
    loss_value = loss_cols[0, 0] / (lax.axis_size("dp") * MB * out_width)
    return (grad_layers, grad_head, loss_value)


def solution(mesh):
    in_specs = (
        P(("dp", "mp"), None),
        P(("dp", "mp"), None, None),
        P(("dp", "mp"), None),
        P(("dp", "mp"), None, None),
        P(("dp", "mp"), None),
        P(("dp", "mp"), None),
        P(),
        P("section", "mp", None),
        P(),
    )
    out_specs = (P("section", ("dp", "mp"), None), P(("dp", "mp"), "section"), P())
    return jax.shard_map(local, mesh=mesh, in_specs=in_specs, out_specs=out_specs, check_vma=False)
```

profile of v0, /device:TPU:4, one launch (start us, length us, event | category | flops | bytes accessed | tf_op | source)
XLA Modules:
  0.0 672.2 jit_solution(17826597853342746980)
XLA Ops:
  10.1 36.6 %psum.7 = f32[6]{0:T(128)S(1)} all-reduce(f32[6]{0:T(128)S(1)} %gather_fusion), channel_id=1, replica_groups=mesh['dp'=2,'section'=8,'mp'=16] {'mp'}, use_global_device_ids=true, to_apply=%region_7.0 | all-reduce | flops 6 | bytes 48 | tf_op jit(solution)/shard_map/psum | solution.py:89
  46.7 42.4 %all-gather.3.cloned.1.call-done = bf16[1,2048,2048]{2,1,0:T(8,128)(2,1)} async-done(((bf16[1,128,2048]{2,1,0:T(8,128)(2,1)}), bf16[1,2048,2048]{2,1,0:T(8,128)(2,1)}) %all-gather.3.cloned.1.call-update) | async-done | bytes 8388624 | tf_op jit(solution)/shard_map/all_gather | solution.py:83
  89.4 174.7 %while.49 = (s32[]{:T(128)}, bf16[1,33,2048]{2,1,0:T(8,128)(2,1)S(1)}, bf16[6,1,33,2048]{3,2,1,0:T(8,128)(2,1)S(1)}, bf16[6,1,33,2048]{3,2,1,0:T(8,128)(2,1)S(1)...) while((s32[]{:T(128)}, ...), condition=%wide.region_5.0_spmd, body=%wide.region_0.5_spmd.sunk | while | flops 346843136 | bytes 14290341 | solution.py:130
  89.5 6.7 conditional.10
  96.2 5.1 conditional.11
  106.2 6.7 conditional.10
  112.9 5.1 conditional.11
  122.4 6.7 conditional.10
  129.1 5.1 conditional.11
  138.3 6.7 conditional.10
  145.1 5.1 conditional.11
  145.1 4.9 convolution_bitcast_fusion
  154.3 6.7 conditional.10
  161.1 5.1 conditional.11
  170.3 6.7 conditional.10
  177.0 5.1 conditional.11
  186.3 6.7 conditional.10
  198.7 6.7 conditional.10
  209.6 6.7 conditional.10
  220.5 6.7 conditional.10
  231.4 6.7 conditional.10
  242.3 6.7 conditional.10
  253.2 6.7 conditional.10
  265.3 276.2 %while.50 = (s32[]{:T(128)}, bf16[1,33,2048]{2,1,0:T(8,128)(2,1)S(1)}, bf16[6,1,33,2048]{3,2,1,0:T(8,128)(2,1)}, bf16[6,1,33,1024]{3,2,1,0:T(8,128)(2,1)S(1)}, f...) while((s32[]{:T(128)}, ...), condition=%wide.region_15.16_spmd, body=%wide.region_8.15_spmd.sunk | while | flops 832231424 | bytes 80654912 | solution.py:196
  293.3 5.2 collective-permute-done.1
  317.9 73.0 %collective-permute-done.1 = bf16[1,33,2048]{2,1,0:T(8,128)(2,1)S(1)} collective-permute-done((bf16[1,33,2048]{2,1,0:T(8,128)(2,1)S(1)}, bf16[1,33,2048]{2,1,0:T(8,128)(2,1)S(1)}, u32[]{:S(2)}, u32[]{:S(2)}) %collective-permute-start.1) | collective-permute-done | bytes 135200 | tf_op jit(solution)/shard_map/while/body/eval_jaxpr/ppermute | solution.py:12
  391.6 8.5 %conditional.13 = (bf16[1,33,2048]{2,1,0:T(8,128)(2,1)S(1)}, bf16[1,33,2048]{2,1,0:T(8,128)(2,1)S(1)}) conditional(s32[]{:T(128)} %convert_element_type.144, bf16[1,33,2048]{2,1,0:T(8,128)(2,1)S(1)} %get-tuple-element.973, (bf16[1,33,2048]{2,1,0:T(8,128)(2,1)S(1)}, s32[]{:T(128)}, bf16[6,1,33,2048]{3,2,1,0:T(8,128)(2,1)S(1)}, ...), branch_computations={%region_12.12_spmd, %region_13.14_spmd} | conditional | flops 554866688 | bytes 53235792 | solution.py:183
  391.6 5.1 convolution_bitcast_fusion.2
  403.9 13.5 %collective-permute-done.1 = bf16[1,33,2048]{2,1,0:T(8,128)(2,1)S(1)} collective-permute-done((bf16[1,33,2048]{2,1,0:T(8,128)(2,1)S(1)}, bf16[1,33,2048]{2,1,0:T(8,128)(2,1)S(1)}, u32[]{:S(2)}, u32[]{:S(2)}) %collective-permute-start.1) | collective-permute-done | bytes 135200 | tf_op jit(solution)/shard_map/while/body/eval_jaxpr/ppermute | solution.py:12
  418.1 8.5 %conditional.13 = (bf16[1,33,2048]{2,1,0:T(8,128)(2,1)S(1)}, bf16[1,33,2048]{2,1,0:T(8,128)(2,1)S(1)}) conditional(s32[]{:T(128)} %convert_element_type.144, bf16[1,33,2048]{2,1,0:T(8,128)(2,1)S(1)} %get-tuple-element.973, (bf16[1,33,2048]{2,1,0:T(8,128)(2,1)S(1)}, s32[]{:T(128)}, bf16[6,1,33,2048]{3,2,1,0:T(8,128)(2,1)S(1)}, ...), branch_computations={%region_12.12_spmd, %region_13.14_spmd} | conditional | flops 554866688 | bytes 53235792 | solution.py:183
  418.1 5.1 convolution_bitcast_fusion.2
  430.5 13.6 %collective-permute-done.1 = bf16[1,33,2048]{2,1,0:T(8,128)(2,1)S(1)} collective-permute-done((bf16[1,33,2048]{2,1,0:T(8,128)(2,1)S(1)}, bf16[1,33,2048]{2,1,0:T(8,128)(2,1)S(1)}, u32[]{:S(2)}, u32[]{:S(2)}) %collective-permute-start.1) | collective-permute-done | bytes 135200 | tf_op jit(solution)/shard_map/while/body/eval_jaxpr/ppermute | solution.py:12
  444.7 8.5 %conditional.13 = (bf16[1,33,2048]{2,1,0:T(8,128)(2,1)S(1)}, bf16[1,33,2048]{2,1,0:T(8,128)(2,1)S(1)}) conditional(s32[]{:T(128)} %convert_element_type.144, bf16[1,33,2048]{2,1,0:T(8,128)(2,1)S(1)} %get-tuple-element.973, (bf16[1,33,2048]{2,1,0:T(8,128)(2,1)S(1)}, s32[]{:T(128)}, bf16[6,1,33,2048]{3,2,1,0:T(8,128)(2,1)S(1)}, ...), branch_computations={%region_12.12_spmd, %region_13.14_spmd} | conditional | flops 554866688 | bytes 53235792 | solution.py:183
  444.7 5.1 convolution_bitcast_fusion.2
  457.0 13.5 %collective-permute-done.1 = bf16[1,33,2048]{2,1,0:T(8,128)(2,1)S(1)} collective-permute-done((bf16[1,33,2048]{2,1,0:T(8,128)(2,1)S(1)}, bf16[1,33,2048]{2,1,0:T(8,128)(2,1)S(1)}, u32[]{:S(2)}, u32[]{:S(2)}) %collective-permute-start.1) | collective-permute-done | bytes 135200 | tf_op jit(solution)/shard_map/while/body/eval_jaxpr/ppermute | solution.py:12
  471.2 8.5 %conditional.13 = (bf16[1,33,2048]{2,1,0:T(8,128)(2,1)S(1)}, bf16[1,33,2048]{2,1,0:T(8,128)(2,1)S(1)}) conditional(s32[]{:T(128)} %convert_element_type.144, bf16[1,33,2048]{2,1,0:T(8,128)(2,1)S(1)} %get-tuple-element.973, (bf16[1,33,2048]{2,1,0:T(8,128)(2,1)S(1)}, s32[]{:T(128)}, bf16[6,1,33,2048]{3,2,1,0:T(8,128)(2,1)S(1)}, ...), branch_computations={%region_12.12_spmd, %region_13.14_spmd} | conditional | flops 554866688 | bytes 53235792 | solution.py:183
  471.2 5.1 convolution_bitcast_fusion.2
  483.6 13.5 %collective-permute-done.1 = bf16[1,33,2048]{2,1,0:T(8,128)(2,1)S(1)} collective-permute-done((bf16[1,33,2048]{2,1,0:T(8,128)(2,1)S(1)}, bf16[1,33,2048]{2,1,0:T(8,128)(2,1)S(1)}, u32[]{:S(2)}, u32[]{:S(2)}) %collective-permute-start.1) | collective-permute-done | bytes 135200 | tf_op jit(solution)/shard_map/while/body/eval_jaxpr/ppermute | solution.py:12
  497.8 8.5 %conditional.13 = (bf16[1,33,2048]{2,1,0:T(8,128)(2,1)S(1)}, bf16[1,33,2048]{2,1,0:T(8,128)(2,1)S(1)}) conditional(s32[]{:T(128)} %convert_element_type.144, bf16[1,33,2048]{2,1,0:T(8,128)(2,1)S(1)} %get-tuple-element.973, (bf16[1,33,2048]{2,1,0:T(8,128)(2,1)S(1)}, s32[]{:T(128)}, bf16[6,1,33,2048]{3,2,1,0:T(8,128)(2,1)S(1)}, ...), branch_computations={%region_12.12_spmd, %region_13.14_spmd} | conditional | flops 554866688 | bytes 53235792 | solution.py:183
  497.8 5.1 convolution_bitcast_fusion.2
  510.2 15.0 %collective-permute-done.1 = bf16[1,33,2048]{2,1,0:T(8,128)(2,1)S(1)} collective-permute-done((bf16[1,33,2048]{2,1,0:T(8,128)(2,1)S(1)}, bf16[1,33,2048]{2,1,0:T(8,128)(2,1)S(1)}, u32[]{:S(2)}, u32[]{:S(2)}) %collective-permute-start.1) | collective-permute-done | bytes 135200 | tf_op jit(solution)/shard_map/while/body/eval_jaxpr/ppermute | solution.py:12
  525.8 8.5 %conditional.13 = (bf16[1,33,2048]{2,1,0:T(8,128)(2,1)S(1)}, bf16[1,33,2048]{2,1,0:T(8,128)(2,1)S(1)}) conditional(s32[]{:T(128)} %convert_element_type.144, bf16[1,33,2048]{2,1,0:T(8,128)(2,1)S(1)} %get-tuple-element.973, (bf16[1,33,2048]{2,1,0:T(8,128)(2,1)S(1)}, s32[]{:T(128)}, bf16[6,1,33,2048]{3,2,1,0:T(8,128)(2,1)S(1)}, ...), branch_computations={%region_12.12_spmd, %region_13.14_spmd} | conditional | flops 554866688 | bytes 53235792 | solution.py:183
  525.8 5.1 convolution_bitcast_fusion.2
  541.5 6.8 %bitcast_convert_fusion = bf16[2048,2048]{1,0:T(8,128)(2,1)} fusion(bf16[6,1,33,2048]{3,2,1,0:T(8,128)(2,1)} %get-tuple-element.662, bf16[6,1,33,2048]{3,2,1,0:T(8,128)(2,1)S(1)} %get-tuple-element.1109), kind=kOutput, calls=%fused_computation.68 | convolution fusion | flops 1665138688 | bytes 10010624 | tf_op jit(solution)/shard_map/dot_general | solution.py:203
  549.0 5.9 all-to-all-start.2
  560.0 6.8 %all-to-all-start = ((bf16[32,64,1024]{2,1,0:T(8,128)(2,1)}), bf16[32,64,1024]{2,1,0:T(8,128)(2,1)}, u32[]{:S(2)}, u32[]{:S(2)}) async-start(bf16[32,64,1024]{2,1,0:T(8,128)(2,1)} %bitcast.121), calls=%async_computation.1 | async-start | bytes 8388608 | tf_op jit(solution)/shard_map/all_to_all | solution.py:22
  567.5 69.4 %all-to-all-done = bf16[32,64,1024]{2,1,0:T(8,128)(2,1)} async-done(((bf16[32,64,1024]{2,1,0:T(8,128)(2,1)}), bf16[32,64,1024]{2,1,0:T(8,128)(2,1)}, u32[]{:S(2)}, u32[]{:S(2)}) %all-to-all-start) | async-done | bytes 4194336 | tf_op jit(solution)/shard_map/all_to_all | solution.py:22
  653.9 8.0 %all-to-all-done.1 = bf16[8,64,128]{2,1,0:T(8,128)(2,1)S(1)} async-done(((bf16[8,64,128]{2,1,0:T(8,128)(2,1)}), bf16[8,64,128]{2,1,0:T(8,128)(2,1)S(1)}, u32[]{:S(2)}, u32[]{:S(2)}) %all-to-all-start.1) | async-done | bytes 131104 | tf_op jit(solution)/shard_map/all_to_all | solution.py:22
  (377 shorter events, 282.5 us)
Async XLA Ops:
  7.2 82.0 %all-gather.3.cloned.1.call-start = ((), (), s32[]{:S(2)}) async-start(), calls=%async_computation.6 | async-start | bytes 8912896 | tf_op jit(solution)/shard_map/all_gather | solution.py:83
  7.9 654.5 %reduce-scatter.2.cloned.1.call-start = ((), (), s32[]{:S(2)}) async-start(), calls=%async_computation.5 | async-start | bytes 8650752 | tf_op jit(solution)/shard_map/reduce_scatter | solution.py:202
  101.3 4.9 collective-permute-start
  118.0 4.3 collective-permute-start
  134.2 4.1 collective-permute-start
  150.2 4.1 collective-permute-start
  166.2 4.1 collective-permute-start
  182.2 4.1 collective-permute-start
  193.1 5.6 collective-permute-start
  205.5 4.1 collective-permute-start
  216.4 4.1 collective-permute-start
  227.3 4.1 collective-permute-start
  238.2 4.1 collective-permute-start
  249.1 4.1 collective-permute-start
  260.0 4.1 collective-permute-start
  266.1 7.7 %collective-permute-start.1 = (bf16[1,33,2048]{2,1,0:T(8,128)(2,1)S(1)}, bf16[1,33,2048]{2,1,0:T(8,128)(2,1)S(1)}, u32[]{:S(2)}, u32[]{:S(2)}) collective-permute-start(bf16[1,33,2048]{2,1,0:T(8,128)(2,1)S(1)} %get-tuple-element.974), channel_id=1, source_target_pairs={{16,0},{32,16},{48,32},{64,48},{80,64},{96,80},{112,96},{17,1},{33... | collective-permute-start | bytes 405512 | tf_op jit(solution)/shard_map/while/body/eval_jaxpr/ppermute | solution.py:12
  274.4 7.2 %collective-permute-start.1 = (bf16[1,33,2048]{2,1,0:T(8,128)(2,1)S(1)}, bf16[1,33,2048]{2,1,0:T(8,128)(2,1)S(1)}, u32[]{:S(2)}, u32[]{:S(2)}) collective-permute-start(bf16[1,33,2048]{2,1,0:T(8,128)(2,1)S(1)} %get-tuple-element.974), channel_id=1, source_target_pairs={{16,0},{32,16},{48,32},{64,48},{80,64},{96,80},{112,96},{17,1},{33... | collective-permute-start | bytes 405512 | tf_op jit(solution)/shard_map/while/body/eval_jaxpr/ppermute | solution.py:12
  282.3 7.2 %collective-permute-start.1 = (bf16[1,33,2048]{2,1,0:T(8,128)(2,1)S(1)}, bf16[1,33,2048]{2,1,0:T(8,128)(2,1)S(1)}, u32[]{:S(2)}, u32[]{:S(2)}) collective-permute-start(bf16[1,33,2048]{2,1,0:T(8,128)(2,1)S(1)} %get-tuple-element.974), channel_id=1, source_target_pairs={{16,0},{32,16},{48,32},{64,48},{80,64},{96,80},{112,96},{17,1},{33... | collective-permute-start | bytes 405512 | tf_op jit(solution)/shard_map/while/body/eval_jaxpr/ppermute | solution.py:12
  290.2 8.2 %collective-permute-start.1 = (bf16[1,33,2048]{2,1,0:T(8,128)(2,1)S(1)}, bf16[1,33,2048]{2,1,0:T(8,128)(2,1)S(1)}, u32[]{:S(2)}, u32[]{:S(2)}) collective-permute-start(bf16[1,33,2048]{2,1,0:T(8,128)(2,1)S(1)} %get-tuple-element.974), channel_id=1, source_target_pairs={{16,0},{32,16},{48,32},{64,48},{80,64},{96,80},{112,96},{17,1},{33... | collective-permute-start | bytes 405512 | tf_op jit(solution)/shard_map/while/body/eval_jaxpr/ppermute | solution.py:12
  299.1 7.2 %collective-permute-start.1 = (bf16[1,33,2048]{2,1,0:T(8,128)(2,1)S(1)}, bf16[1,33,2048]{2,1,0:T(8,128)(2,1)S(1)}, u32[]{:S(2)}, u32[]{:S(2)}) collective-permute-start(bf16[1,33,2048]{2,1,0:T(8,128)(2,1)S(1)} %get-tuple-element.974), channel_id=1, source_target_pairs={{16,0},{32,16},{48,32},{64,48},{80,64},{96,80},{112,96},{17,1},{33... | collective-permute-start | bytes 405512 | tf_op jit(solution)/shard_map/while/body/eval_jaxpr/ppermute | solution.py:12
  307.0 7.2 %collective-permute-start.1 = (bf16[1,33,2048]{2,1,0:T(8,128)(2,1)S(1)}, bf16[1,33,2048]{2,1,0:T(8,128)(2,1)S(1)}, u32[]{:S(2)}, u32[]{:S(2)}) collective-permute-start(bf16[1,33,2048]{2,1,0:T(8,128)(2,1)S(1)} %get-tuple-element.974), channel_id=1, source_target_pairs={{16,0},{32,16},{48,32},{64,48},{80,64},{96,80},{112,96},{17,1},{33... | collective-permute-start | bytes 405512 | tf_op jit(solution)/shard_map/while/body/eval_jaxpr/ppermute | solution.py:12
  314.9 76.0 %collective-permute-start.1 = (bf16[1,33,2048]{2,1,0:T(8,128)(2,1)S(1)}, bf16[1,33,2048]{2,1,0:T(8,128)(2,1)S(1)}, u32[]{:S(2)}, u32[]{:S(2)}) collective-permute-start(bf16[1,33,2048]{2,1,0:T(8,128)(2,1)S(1)} %get-tuple-element.974), channel_id=1, source_target_pairs={{16,0},{32,16},{48,32},{64,48},{80,64},{96,80},{112,96},{17,1},{33... | collective-permute-start | bytes 405512 | tf_op jit(solution)/shard_map/while/body/eval_jaxpr/ppermute | solution.py:12
  391.6 5.8 copy-start
  400.0 17.4 %collective-permute-start.1 = (bf16[1,33,2048]{2,1,0:T(8,128)(2,1)S(1)}, bf16[1,33,2048]{2,1,0:T(8,128)(2,1)S(1)}, u32[]{:S(2)}, u32[]{:S(2)}) collective-permute-start(bf16[1,33,2048]{2,1,0:T(8,128)(2,1)S(1)} %get-tuple-element.974), channel_id=1, source_target_pairs={{16,0},{32,16},{48,32},{64,48},{80,64},{96,80},{112,96},{17,1},{33... | collective-permute-start | bytes 405512 | tf_op jit(solution)/shard_map/while/body/eval_jaxpr/ppermute | solution.py:12
  418.1 5.8 copy-start
  426.6 17.4 %collective-permute-start.1 = (bf16[1,33,2048]{2,1,0:T(8,128)(2,1)S(1)}, bf16[1,33,2048]{2,1,0:T(8,128)(2,1)S(1)}, u32[]{:S(2)}, u32[]{:S(2)}) collective-permute-start(bf16[1,33,2048]{2,1,0:T(8,128)(2,1)S(1)} %get-tuple-element.974), channel_id=1, source_target_pairs={{16,0},{32,16},{48,32},{64,48},{80,64},{96,80},{112,96},{17,1},{33... | collective-permute-start | bytes 405512 | tf_op jit(solution)/shard_map/while/body/eval_jaxpr/ppermute | solution.py:12
  444.7 5.8 copy-start
  453.2 17.4 %collective-permute-start.1 = (bf16[1,33,2048]{2,1,0:T(8,128)(2,1)S(1)}, bf16[1,33,2048]{2,1,0:T(8,128)(2,1)S(1)}, u32[]{:S(2)}, u32[]{:S(2)}) collective-permute-start(bf16[1,33,2048]{2,1,0:T(8,128)(2,1)S(1)} %get-tuple-element.974), channel_id=1, source_target_pairs={{16,0},{32,16},{48,32},{64,48},{80,64},{96,80},{112,96},{17,1},{33... | collective-permute-start | bytes 405512 | tf_op jit(solution)/shard_map/while/body/eval_jaxpr/ppermute | solution.py:12
  471.2 5.8 copy-start
  479.7 17.4 %collective-permute-start.1 = (bf16[1,33,2048]{2,1,0:T(8,128)(2,1)S(1)}, bf16[1,33,2048]{2,1,0:T(8,128)(2,1)S(1)}, u32[]{:S(2)}, u32[]{:S(2)}) collective-permute-start(bf16[1,33,2048]{2,1,0:T(8,128)(2,1)S(1)} %get-tuple-element.974), channel_id=1, source_target_pairs={{16,0},{32,16},{48,32},{64,48},{80,64},{96,80},{112,96},{17,1},{33... | collective-permute-start | bytes 405512 | tf_op jit(solution)/shard_map/while/body/eval_jaxpr/ppermute | solution.py:12
  497.8 5.8 copy-start
  506.3 18.9 %collective-permute-start.1 = (bf16[1,33,2048]{2,1,0:T(8,128)(2,1)S(1)}, bf16[1,33,2048]{2,1,0:T(8,128)(2,1)S(1)}, u32[]{:S(2)}, u32[]{:S(2)}) collective-permute-start(bf16[1,33,2048]{2,1,0:T(8,128)(2,1)S(1)} %get-tuple-element.974), channel_id=1, source_target_pairs={{16,0},{32,16},{48,32},{64,48},{80,64},{96,80},{112,96},{17,1},{33... | collective-permute-start | bytes 405512 | tf_op jit(solution)/shard_map/while/body/eval_jaxpr/ppermute | solution.py:12
  525.8 5.8 copy-start
  534.3 7.2 %collective-permute-start.1 = (bf16[1,33,2048]{2,1,0:T(8,128)(2,1)S(1)}, bf16[1,33,2048]{2,1,0:T(8,128)(2,1)S(1)}, u32[]{:S(2)}, u32[]{:S(2)}) collective-permute-start(bf16[1,33,2048]{2,1,0:T(8,128)(2,1)S(1)} %get-tuple-element.974), channel_id=1, source_target_pairs={{16,0},{32,16},{48,32},{64,48},{80,64},{96,80},{112,96},{17,1},{33... | collective-permute-start | bytes 405512 | tf_op jit(solution)/shard_map/while/body/eval_jaxpr/ppermute | solution.py:12
  549.0 11.1 %all-to-all-start.2 = ((f32[32,1,1]{2,1,0:T(1,128)}), f32[32,1,1]{2,1,0:T(1,128)S(1)}, u32[]{:S(2)}, u32[]{:S(2)}) async-start(f32[32,1,1]{2,1,0:T(1,128)} %broadcast_in_dim.76), calls=%async_computation.3 | async-start | bytes 32768 | tf_op jit(solution)/shard_map/all_to_all | solution.py:28
  560.0 76.8 %all-to-all-start = ((bf16[32,64,1024]{2,1,0:T(8,128)(2,1)}), bf16[32,64,1024]{2,1,0:T(8,128)(2,1)}, u32[]{:S(2)}, u32[]{:S(2)}) async-start(bf16[32,64,1024]{2,1,0:T(8,128)(2,1)} %bitcast.121), calls=%async_computation.1 | async-start | bytes 8388608 | tf_op jit(solution)/shard_map/all_to_all | solution.py:22
  638.1 10.9 %all-to-all-start.3 = ((bf16[8,1,1]{2,1,0:T(2,128)(2,1)}), bf16[8,1,1]{2,1,0:T(2,128)(2,1)S(1)}, u32[]{:S(2)}, u32[]{:S(2)}) async-start(bf16[8,1,1]{2,1,0:T(2,128)(2,1)} %transpose_reshape.3), calls=%async_computation.4 | async-start | bytes 8192 | tf_op jit(solution)/shard_map/all_to_all | solution.py:22
  649.0 12.8 %all-to-all-start.1 = ((bf16[8,64,128]{2,1,0:T(8,128)(2,1)}), bf16[8,64,128]{2,1,0:T(8,128)(2,1)S(1)}, u32[]{:S(2)}, u32[]{:S(2)}) async-start(bf16[8,64,128]{2,1,0:T(8,128)(2,1)} %copy.31), calls=%async_computation.2 | async-start | bytes 262144 | tf_op jit(solution)/shard_map/all_to_all | solution.py:22
Sparse Core Ops, SparseCore 0:
  10.4 78.7 all-gather.2
  548.5 106.9 reduce-scatter.1
where the time goes:
time: 676 us; the launch traced here: 672 us
  waiting for transfers between devices  334 us (49%)
  matrix products  109 us (16%)
  local copies, waits for them, and re-layouts  67.7 us (10%)
  starting transfers between devices  54.7 us (8%)
  blocking collectives  36.6 us (5%)
  other arithmetic  27.2 us (4%)
  loops' own time  26.6 us (4%)
  between operations  15.9 us (2%)
    ppermute x26, waiting for transfers between devices, from_behind(): lax.ppermute(value, axis, [(source, source + steps) for source in range(i...  208 us
    all_to_all x3, waiting for transfers between devices, sent_and_summed(): lax.all_to_all(parts, axis, split_axis=0, concat_axis=0, tiled=True)  80.9 us
    all_gather x1, waiting for transfers between devices, local(): layer_full = lax.all_gather(layers[0], 'mp', axis=0, tiled=True)  42.4 us
    psum x1, blocking collectives, local(): lax.psum(jnp.sum(sample_total[sample_order].reshape(MB, per_batch), axis=...  36.6 us
    ppermute x26, starting transfers between devices, from_behind(): lax.ppermute(value, axis, [(source, source + steps) for source in range(i...  35.2 us
    dot_general x6, matrix products, backward_active(): jnp.dot(row_block.reshape(-1, model_width), layer_full, preferred_element...  30.4 us
    dot_general x6, matrix products, forward_layer(): jnp.dot(row_block.reshape(-1, model_width), weight, preferred_element_typ...  29.5 us
    dot_general x13, matrix products, lift_batch(): jnp.dot(rows_in.reshape(-1, in_width), encoder, preferred_element_type=jn...  26.7 us
  transfers between devices with their start and end apart: 32, of which 31 were waited for; matrix products, arithmetic and copies ran while one was open for 6% of the time, Pallas kernels for 0%

commit v1 on v0

--- a/solution.py
+++ b/solution.py
@@ -86,8 +86,9 @@
         [jnp.ones((samp_dev, 1), jnp.float32), rank_mask.astype(jnp.float32)], axis=1
     )
     sample_total = jnp.sum(row_weight, axis=1)
-    batch_counts = lax.psum(
-        jnp.sum(sample_total[sample_order].reshape(MB, per_batch), axis=1), "mp"
+    batch_counts = jnp.sum(
+        lax.all_gather(jnp.sum(sample_total[sample_order].reshape(MB, per_batch), axis=1), "mp"),
+        axis=0,
     )
 
     def picked_of(batch_slot):

time: 676 us -> 678 us (level)
    unnamed x0 -> x1, blocking collectives: none -> 36.7 us
    psum x1 -> x0, blocking collectives: 36.6 us -> none  [local(): lax.psum(jnp.sum(sample_total[sample_order].reshape(MB, per_batch), axis=...]
where the time goes in v1:
time: 678 us; the launch traced here: 674 us
  waiting for transfers between devices  334 us (49%)
  matrix products  109 us (16%)
  local copies, waits for them, and re-layouts  69.3 us (10%)
  starting transfers between devices  54.7 us (8%)
  blocking collectives  36.7 us (5%)
  other arithmetic  27.3 us (4%)
  loops' own time  26.5 us (4%)
  between operations  16.6 us (2%)
    ppermute x26, waiting for transfers between devices, from_behind(): lax.ppermute(value, axis, [(source, source + steps) for source in range(i...  209 us
    all_to_all x3, waiting for transfers between devices, sent_and_summed(): lax.all_to_all(parts, axis, split_axis=0, concat_axis=0, tiled=True)  80.9 us
    all_gather x1, waiting for transfers between devices, local(): layer_full = lax.all_gather(layers[0], 'mp', axis=0, tiled=True)  40 us
    unnamed x1, blocking collectives  36.7 us
    ppermute x26, starting transfers between devices, from_behind(): lax.ppermute(value, axis, [(source, source + steps) for source in range(i...  35.2 us
    dot_general x6, matrix products, backward_active(): jnp.dot(row_block.reshape(-1, model_width), layer_full, preferred_element...  30.4 us
    dot_general x6, matrix products, forward_layer(): jnp.dot(row_block.reshape(-1, model_width), weight, preferred_element_typ...  29.5 us
    dot_general x13, matrix products, lift_batch(): jnp.dot(rows_in.reshape(-1, in_width), encoder, preferred_element_type=jn...  26.7 us
  transfers between devices with their start and end apart: 32, of which 31 were waited for; matrix products, arithmetic and copies ran while one was open for 6% of the time, Pallas kernels for 0%

profile of v1, /device:TPU:4, one launch (start us, length us, event | category | flops | bytes accessed | tf_op | source)
XLA Modules:
  0.0 673.8 jit_solution(1165200505410530941)
XLA Ops:
  12.4 36.7 %all-reduce.1 = f32[96]{0:T(128)S(1)} all-reduce(f32[96]{0:T(128)S(1)} %dynamic-update-slice.5), channel_id=3, replica_groups=mesh['dp'=2,'section'=8,'mp'=16] {'mp'}, use_global_device_ids=true, to_apply=%add.1 | all-reduce | flops 96 | bytes 768
  49.2 40.0 %all-gather.4.cloned.1.call-done = bf16[1,2048,2048]{2,1,0:T(8,128)(2,1)} async-done(((bf16[1,128,2048]{2,1,0:T(8,128)(2,1)}), bf16[1,2048,2048]{2,1,0:T(8,128)(2,1)}) %all-gather.4.cloned.1.call-update) | async-done | bytes 8388624 | tf_op jit(solution)/shard_map/all_gather | solution.py:83
  89.4 174.6 %while.49 = (s32[]{:T(128)}, bf16[1,33,2048]{2,1,0:T(8,128)(2,1)S(1)}, bf16[6,1,33,2048]{3,2,1,0:T(8,128)(2,1)S(1)}, bf16[6,1,33,2048]{3,2,1,0:T(8,128)(2,1)S(1)...) while((s32[]{:T(128)}, ...), condition=%wide.region_5.0_spmd, body=%wide.region_0.5_spmd.sunk | while | flops 346843136 | bytes 14290341 | solution.py:131
  89.5 6.7 conditional.10
  96.2 5.1 conditional.11
  106.2 6.7 conditional.10
  112.9 5.1 conditional.11
  122.3 6.7 conditional.10
  129.0 5.1 conditional.11
  138.3 6.7 conditional.10
  145.0 5.1 conditional.11
  145.0 4.9 convolution_bitcast_fusion
  154.3 6.7 conditional.10
  161.0 5.1 conditional.11
  170.3 6.7 conditional.10
  177.0 5.1 conditional.11
  186.2 6.7 conditional.10
  198.6 6.7 conditional.10
  209.5 6.7 conditional.10
  220.4 6.7 conditional.10
  231.3 6.7 conditional.10
  242.2 6.7 conditional.10
  253.1 6.7 conditional.10
  265.2 277.9 %while.50 = (s32[]{:T(128)}, bf16[1,33,2048]{2,1,0:T(8,128)(2,1)S(1)}, bf16[6,1,33,2048]{3,2,1,0:T(8,128)(2,1)}, bf16[6,1,33,1024]{3,2,1,0:T(8,128)(2,1)S(1)}, f...) while((s32[]{:T(128)}, ...), condition=%wide.region_15.16_spmd, body=%wide.region_8.15_spmd.sunk | while | flops 832231424 | bytes 80654912 | solution.py:197
  293.2 5.2 collective-permute-done.1
  317.8 73.3 %collective-permute-done.1 = bf16[1,33,2048]{2,1,0:T(8,128)(2,1)S(1)} collective-permute-done((bf16[1,33,2048]{2,1,0:T(8,128)(2,1)S(1)}, bf16[1,33,2048]{2,1,0:T(8,128)(2,1)S(1)}, u32[]{:S(2)}, u32[]{:S(2)}) %collective-permute-start.1) | collective-permute-done | bytes 135200 | tf_op jit(solution)/shard_map/while/body/eval_jaxpr/ppermute | solution.py:12
  391.8 8.5 %conditional.13 = (bf16[1,33,2048]{2,1,0:T(8,128)(2,1)S(1)}, bf16[1,33,2048]{2,1,0:T(8,128)(2,1)S(1)}) conditional(s32[]{:T(128)} %convert_element_type.144, bf16[1,33,2048]{2,1,0:T(8,128)(2,1)S(1)} %get-tuple-element.973, (bf16[1,33,2048]{2,1,0:T(8,128)(2,1)S(1)}, s32[]{:T(128)}, bf16[6,1,33,2048]{3,2,1,0:T(8,128)(2,1)S(1)}, ...), branch_computations={%region_12.12_spmd, %region_13.14_spmd} | conditional | flops 554866688 | bytes 53235792 | solution.py:184
  391.8 5.1 convolution_bitcast_fusion.2
  404.2 13.8 %collective-permute-done.1 = bf16[1,33,2048]{2,1,0:T(8,128)(2,1)S(1)} collective-permute-done((bf16[1,33,2048]{2,1,0:T(8,128)(2,1)S(1)}, bf16[1,33,2048]{2,1,0:T(8,128)(2,1)S(1)}, u32[]{:S(2)}, u32[]{:S(2)}) %collective-permute-start.1) | collective-permute-done | bytes 135200 | tf_op jit(solution)/shard_map/while/body/eval_jaxpr/ppermute | solution.py:12
  418.6 8.5 %conditional.13 = (bf16[1,33,2048]{2,1,0:T(8,128)(2,1)S(1)}, bf16[1,33,2048]{2,1,0:T(8,128)(2,1)S(1)}) conditional(s32[]{:T(128)} %convert_element_type.144, bf16[1,33,2048]{2,1,0:T(8,128)(2,1)S(1)} %get-tuple-element.973, (bf16[1,33,2048]{2,1,0:T(8,128)(2,1)S(1)}, s32[]{:T(128)}, bf16[6,1,33,2048]{3,2,1,0:T(8,128)(2,1)S(1)}, ...), branch_computations={%region_12.12_spmd, %region_13.14_spmd} | conditional | flops 554866688 | bytes 53235792 | solution.py:184
  418.6 5.1 convolution_bitcast_fusion.2
  431.0 13.8 %collective-permute-done.1 = bf16[1,33,2048]{2,1,0:T(8,128)(2,1)S(1)} collective-permute-done((bf16[1,33,2048]{2,1,0:T(8,128)(2,1)S(1)}, bf16[1,33,2048]{2,1,0:T(8,128)(2,1)S(1)}, u32[]{:S(2)}, u32[]{:S(2)}) %collective-permute-start.1) | collective-permute-done | bytes 135200 | tf_op jit(solution)/shard_map/while/body/eval_jaxpr/ppermute | solution.py:12
  445.5 8.5 %conditional.13 = (bf16[1,33,2048]{2,1,0:T(8,128)(2,1)S(1)}, bf16[1,33,2048]{2,1,0:T(8,128)(2,1)S(1)}) conditional(s32[]{:T(128)} %convert_element_type.144, bf16[1,33,2048]{2,1,0:T(8,128)(2,1)S(1)} %get-tuple-element.973, (bf16[1,33,2048]{2,1,0:T(8,128)(2,1)S(1)}, s32[]{:T(128)}, bf16[6,1,33,2048]{3,2,1,0:T(8,128)(2,1)S(1)}, ...), branch_computations={%region_12.12_spmd, %region_13.14_spmd} | conditional | flops 554866688 | bytes 53235792 | solution.py:184
  445.5 5.1 convolution_bitcast_fusion.2
  457.8 13.8 %collective-permute-done.1 = bf16[1,33,2048]{2,1,0:T(8,128)(2,1)S(1)} collective-permute-done((bf16[1,33,2048]{2,1,0:T(8,128)(2,1)S(1)}, bf16[1,33,2048]{2,1,0:T(8,128)(2,1)S(1)}, u32[]{:S(2)}, u32[]{:S(2)}) %collective-permute-start.1) | collective-permute-done | bytes 135200 | tf_op jit(solution)/shard_map/while/body/eval_jaxpr/ppermute | solution.py:12
  472.3 8.5 %conditional.13 = (bf16[1,33,2048]{2,1,0:T(8,128)(2,1)S(1)}, bf16[1,33,2048]{2,1,0:T(8,128)(2,1)S(1)}) conditional(s32[]{:T(128)} %convert_element_type.144, bf16[1,33,2048]{2,1,0:T(8,128)(2,1)S(1)} %get-tuple-element.973, (bf16[1,33,2048]{2,1,0:T(8,128)(2,1)S(1)}, s32[]{:T(128)}, bf16[6,1,33,2048]{3,2,1,0:T(8,128)(2,1)S(1)}, ...), branch_computations={%region_12.12_spmd, %region_13.14_spmd} | conditional | flops 554866688 | bytes 53235792 | solution.py:184
  472.3 5.1 convolution_bitcast_fusion.2
  484.7 13.8 %collective-permute-done.1 = bf16[1,33,2048]{2,1,0:T(8,128)(2,1)S(1)} collective-permute-done((bf16[1,33,2048]{2,1,0:T(8,128)(2,1)S(1)}, bf16[1,33,2048]{2,1,0:T(8,128)(2,1)S(1)}, u32[]{:S(2)}, u32[]{:S(2)}) %collective-permute-start.1) | collective-permute-done | bytes 135200 | tf_op jit(solution)/shard_map/while/body/eval_jaxpr/ppermute | solution.py:12
  499.2 8.5 %conditional.13 = (bf16[1,33,2048]{2,1,0:T(8,128)(2,1)S(1)}, bf16[1,33,2048]{2,1,0:T(8,128)(2,1)S(1)}) conditional(s32[]{:T(128)} %convert_element_type.144, bf16[1,33,2048]{2,1,0:T(8,128)(2,1)S(1)} %get-tuple-element.973, (bf16[1,33,2048]{2,1,0:T(8,128)(2,1)S(1)}, s32[]{:T(128)}, bf16[6,1,33,2048]{3,2,1,0:T(8,128)(2,1)S(1)}, ...), branch_computations={%region_12.12_spmd, %region_13.14_spmd} | conditional | flops 554866688 | bytes 53235792 | solution.py:184
  499.2 5.1 convolution_bitcast_fusion.2
  511.5 15.3 %collective-permute-done.1 = bf16[1,33,2048]{2,1,0:T(8,128)(2,1)S(1)} collective-permute-done((bf16[1,33,2048]{2,1,0:T(8,128)(2,1)S(1)}, bf16[1,33,2048]{2,1,0:T(8,128)(2,1)S(1)}, u32[]{:S(2)}, u32[]{:S(2)}) %collective-permute-start.1) | collective-permute-done | bytes 135200 | tf_op jit(solution)/shard_map/while/body/eval_jaxpr/ppermute | solution.py:12
  527.5 8.5 %conditional.13 = (bf16[1,33,2048]{2,1,0:T(8,128)(2,1)S(1)}, bf16[1,33,2048]{2,1,0:T(8,128)(2,1)S(1)}) conditional(s32[]{:T(128)} %convert_element_type.144, bf16[1,33,2048]{2,1,0:T(8,128)(2,1)S(1)} %get-tuple-element.973, (bf16[1,33,2048]{2,1,0:T(8,128)(2,1)S(1)}, s32[]{:T(128)}, bf16[6,1,33,2048]{3,2,1,0:T(8,128)(2,1)S(1)}, ...), branch_computations={%region_12.12_spmd, %region_13.14_spmd} | conditional | flops 554866688 | bytes 53235792 | solution.py:184
  527.5 5.1 convolution_bitcast_fusion.2
  543.2 6.8 %bitcast_convert_fusion = bf16[2048,2048]{1,0:T(8,128)(2,1)} fusion(bf16[6,1,33,2048]{3,2,1,0:T(8,128)(2,1)} %get-tuple-element.662, bf16[6,1,33,2048]{3,2,1,0:T(8,128)(2,1)S(1)} %get-tuple-element.1109), kind=kOutput, calls=%fused_computation.68 | convolution fusion | flops 1665138688 | bytes 10010624 | tf_op jit(solution)/shard_map/dot_general | solution.py:204
  550.6 5.9 all-to-all-start.2
  561.7 6.8 %all-to-all-start = ((bf16[32,64,1024]{2,1,0:T(8,128)(2,1)}), bf16[32,64,1024]{2,1,0:T(8,128)(2,1)}, u32[]{:S(2)}, u32[]{:S(2)}) async-start(bf16[32,64,1024]{2,1,0:T(8,128)(2,1)} %bitcast.122), calls=%async_computation.1 | async-start | bytes 8388608 | tf_op jit(solution)/shard_map/all_to_all | solution.py:22
  569.1 69.4 %all-to-all-done = bf16[32,64,1024]{2,1,0:T(8,128)(2,1)} async-done(((bf16[32,64,1024]{2,1,0:T(8,128)(2,1)}), bf16[32,64,1024]{2,1,0:T(8,128)(2,1)}, u32[]{:S(2)}, u32[]{:S(2)}) %all-to-all-start) | async-done | bytes 4194336 | tf_op jit(solution)/shard_map/all_to_all | solution.py:22
  655.5 8.0 %all-to-all-done.1 = bf16[8,64,128]{2,1,0:T(8,128)(2,1)S(1)} async-done(((bf16[8,64,128]{2,1,0:T(8,128)(2,1)}), bf16[8,64,128]{2,1,0:T(8,128)(2,1)S(1)}, u32[]{:S(2)}, u32[]{:S(2)}) %all-to-all-start.1) | async-done | bytes 131104 | tf_op jit(solution)/shard_map/all_to_all | solution.py:22
  (382 shorter events, 284.2 us)
Async XLA Ops:
  7.2 82.0 %all-gather.4.cloned.1.call-start = ((), (), s32[]{:S(2)}) async-start(), calls=%async_computation.6 | async-start | bytes 8912896 | tf_op jit(solution)/shard_map/all_gather | solution.py:83
  7.9 656.2 %reduce-scatter.2.cloned.1.call-start = ((), (), s32[]{:S(2)}) async-start(), calls=%async_computation.5 | async-start | bytes 8650752 | tf_op jit(solution)/shard_map/reduce_scatter | solution.py:203
  101.3 4.9 collective-permute-start
  118.0 4.3 collective-permute-start
  134.2 4.1 collective-permute-start
  150.1 4.1 collective-permute-start
  166.1 4.1 collective-permute-start
  182.1 4.1 collective-permute-start
  193.0 5.6 collective-permute-start
  205.4 4.1 collective-permute-start
  216.3 4.1 collective-permute-start
  227.2 4.1 collective-permute-start
  238.1 4.1 collective-permute-start
  249.0 4.1 collective-permute-start
  259.9 4.1 collective-permute-start
  266.0 7.7 %collective-permute-start.1 = (bf16[1,33,2048]{2,1,0:T(8,128)(2,1)S(1)}, bf16[1,33,2048]{2,1,0:T(8,128)(2,1)S(1)}, u32[]{:S(2)}, u32[]{:S(2)}) collective-permute-start(bf16[1,33,2048]{2,1,0:T(8,128)(2,1)S(1)} %get-tuple-element.974), channel_id=1, source_target_pairs={{16,0},{32,16},{48,32},{64,48},{80,64},{96,80},{112,96},{17,1},{33... | collective-permute-start | bytes 405512 | tf_op jit(solution)/shard_map/while/body/eval_jaxpr/ppermute | solution.py:12
  274.3 7.2 %collective-permute-start.1 = (bf16[1,33,2048]{2,1,0:T(8,128)(2,1)S(1)}, bf16[1,33,2048]{2,1,0:T(8,128)(2,1)S(1)}, u32[]{:S(2)}, u32[]{:S(2)}) collective-permute-start(bf16[1,33,2048]{2,1,0:T(8,128)(2,1)S(1)} %get-tuple-element.974), channel_id=1, source_target_pairs={{16,0},{32,16},{48,32},{64,48},{80,64},{96,80},{112,96},{17,1},{33... | collective-permute-start | bytes 405512 | tf_op jit(solution)/shard_map/while/body/eval_jaxpr/ppermute | solution.py:12
  282.2 7.2 %collective-permute-start.1 = (bf16[1,33,2048]{2,1,0:T(8,128)(2,1)S(1)}, bf16[1,33,2048]{2,1,0:T(8,128)(2,1)S(1)}, u32[]{:S(2)}, u32[]{:S(2)}) collective-permute-start(bf16[1,33,2048]{2,1,0:T(8,128)(2,1)S(1)} %get-tuple-element.974), channel_id=1, source_target_pairs={{16,0},{32,16},{48,32},{64,48},{80,64},{96,80},{112,96},{17,1},{33... | collective-permute-start | bytes 405512 | tf_op jit(solution)/shard_map/while/body/eval_jaxpr/ppermute | solution.py:12
  290.1 8.2 %collective-permute-start.1 = (bf16[1,33,2048]{2,1,0:T(8,128)(2,1)S(1)}, bf16[1,33,2048]{2,1,0:T(8,128)(2,1)S(1)}, u32[]{:S(2)}, u32[]{:S(2)}) collective-permute-start(bf16[1,33,2048]{2,1,0:T(8,128)(2,1)S(1)} %get-tuple-element.974), channel_id=1, source_target_pairs={{16,0},{32,16},{48,32},{64,48},{80,64},{96,80},{112,96},{17,1},{33... | collective-permute-start | bytes 405512 | tf_op jit(solution)/shard_map/while/body/eval_jaxpr/ppermute | solution.py:12
  299.0 7.2 %collective-permute-start.1 = (bf16[1,33,2048]{2,1,0:T(8,128)(2,1)S(1)}, bf16[1,33,2048]{2,1,0:T(8,128)(2,1)S(1)}, u32[]{:S(2)}, u32[]{:S(2)}) collective-permute-start(bf16[1,33,2048]{2,1,0:T(8,128)(2,1)S(1)} %get-tuple-element.974), channel_id=1, source_target_pairs={{16,0},{32,16},{48,32},{64,48},{80,64},{96,80},{112,96},{17,1},{33... | collective-permute-start | bytes 405512 | tf_op jit(solution)/shard_map/while/body/eval_jaxpr/ppermute | solution.py:12
  306.9 7.2 %collective-permute-start.1 = (bf16[1,33,2048]{2,1,0:T(8,128)(2,1)S(1)}, bf16[1,33,2048]{2,1,0:T(8,128)(2,1)S(1)}, u32[]{:S(2)}, u32[]{:S(2)}) collective-permute-start(bf16[1,33,2048]{2,1,0:T(8,128)(2,1)S(1)} %get-tuple-element.974), channel_id=1, source_target_pairs={{16,0},{32,16},{48,32},{64,48},{80,64},{96,80},{112,96},{17,1},{33... | collective-permute-start | bytes 405512 | tf_op jit(solution)/shard_map/while/body/eval_jaxpr/ppermute | solution.py:12
  314.8 76.3 %collective-permute-start.1 = (bf16[1,33,2048]{2,1,0:T(8,128)(2,1)S(1)}, bf16[1,33,2048]{2,1,0:T(8,128)(2,1)S(1)}, u32[]{:S(2)}, u32[]{:S(2)}) collective-permute-start(bf16[1,33,2048]{2,1,0:T(8,128)(2,1)S(1)} %get-tuple-element.974), channel_id=1, source_target_pairs={{16,0},{32,16},{48,32},{64,48},{80,64},{96,80},{112,96},{17,1},{33... | collective-permute-start | bytes 405512 | tf_op jit(solution)/shard_map/while/body/eval_jaxpr/ppermute | solution.py:12
  391.8 5.8 copy-start
  400.3 17.7 %collective-permute-start.1 = (bf16[1,33,2048]{2,1,0:T(8,128)(2,1)S(1)}, bf16[1,33,2048]{2,1,0:T(8,128)(2,1)S(1)}, u32[]{:S(2)}, u32[]{:S(2)}) collective-permute-start(bf16[1,33,2048]{2,1,0:T(8,128)(2,1)S(1)} %get-tuple-element.974), channel_id=1, source_target_pairs={{16,0},{32,16},{48,32},{64,48},{80,64},{96,80},{112,96},{17,1},{33... | collective-permute-start | bytes 405512 | tf_op jit(solution)/shard_map/while/body/eval_jaxpr/ppermute | solution.py:12
  418.6 5.8 copy-start
  427.1 17.7 %collective-permute-start.1 = (bf16[1,33,2048]{2,1,0:T(8,128)(2,1)S(1)}, bf16[1,33,2048]{2,1,0:T(8,128)(2,1)S(1)}, u32[]{:S(2)}, u32[]{:S(2)}) collective-permute-start(bf16[1,33,2048]{2,1,0:T(8,128)(2,1)S(1)} %get-tuple-element.974), channel_id=1, source_target_pairs={{16,0},{32,16},{48,32},{64,48},{80,64},{96,80},{112,96},{17,1},{33... | collective-permute-start | bytes 405512 | tf_op jit(solution)/shard_map/while/body/eval_jaxpr/ppermute | solution.py:12
  445.5 5.8 copy-start
  454.0 17.7 %collective-permute-start.1 = (bf16[1,33,2048]{2,1,0:T(8,128)(2,1)S(1)}, bf16[1,33,2048]{2,1,0:T(8,128)(2,1)S(1)}, u32[]{:S(2)}, u32[]{:S(2)}) collective-permute-start(bf16[1,33,2048]{2,1,0:T(8,128)(2,1)S(1)} %get-tuple-element.974), channel_id=1, source_target_pairs={{16,0},{32,16},{48,32},{64,48},{80,64},{96,80},{112,96},{17,1},{33... | collective-permute-start | bytes 405512 | tf_op jit(solution)/shard_map/while/body/eval_jaxpr/ppermute | solution.py:12
  472.3 5.8 copy-start
  480.8 17.7 %collective-permute-start.1 = (bf16[1,33,2048]{2,1,0:T(8,128)(2,1)S(1)}, bf16[1,33,2048]{2,1,0:T(8,128)(2,1)S(1)}, u32[]{:S(2)}, u32[]{:S(2)}) collective-permute-start(bf16[1,33,2048]{2,1,0:T(8,128)(2,1)S(1)} %get-tuple-element.974), channel_id=1, source_target_pairs={{16,0},{32,16},{48,32},{64,48},{80,64},{96,80},{112,96},{17,1},{33... | collective-permute-start | bytes 405512 | tf_op jit(solution)/shard_map/while/body/eval_jaxpr/ppermute | solution.py:12
  499.2 5.8 copy-start
  507.6 19.2 %collective-permute-start.1 = (bf16[1,33,2048]{2,1,0:T(8,128)(2,1)S(1)}, bf16[1,33,2048]{2,1,0:T(8,128)(2,1)S(1)}, u32[]{:S(2)}, u32[]{:S(2)}) collective-permute-start(bf16[1,33,2048]{2,1,0:T(8,128)(2,1)S(1)} %get-tuple-element.974), channel_id=1, source_target_pairs={{16,0},{32,16},{48,32},{64,48},{80,64},{96,80},{112,96},{17,1},{33... | collective-permute-start | bytes 405512 | tf_op jit(solution)/shard_map/while/body/eval_jaxpr/ppermute | solution.py:12
  527.5 5.8 copy-start
  536.0 7.2 %collective-permute-start.1 = (bf16[1,33,2048]{2,1,0:T(8,128)(2,1)S(1)}, bf16[1,33,2048]{2,1,0:T(8,128)(2,1)S(1)}, u32[]{:S(2)}, u32[]{:S(2)}) collective-permute-start(bf16[1,33,2048]{2,1,0:T(8,128)(2,1)S(1)} %get-tuple-element.974), channel_id=1, source_target_pairs={{16,0},{32,16},{48,32},{64,48},{80,64},{96,80},{112,96},{17,1},{33... | collective-permute-start | bytes 405512 | tf_op jit(solution)/shard_map/while/body/eval_jaxpr/ppermute | solution.py:12
  550.6 11.1 %all-to-all-start.2 = ((f32[32,1,1]{2,1,0:T(1,128)}), f32[32,1,1]{2,1,0:T(1,128)S(1)}, u32[]{:S(2)}, u32[]{:S(2)}) async-start(f32[32,1,1]{2,1,0:T(1,128)} %broadcast_in_dim.76), calls=%async_computation.3 | async-start | bytes 32768 | tf_op jit(solution)/shard_map/all_to_all | solution.py:28
  561.7 76.8 %all-to-all-start = ((bf16[32,64,1024]{2,1,0:T(8,128)(2,1)}), bf16[32,64,1024]{2,1,0:T(8,128)(2,1)}, u32[]{:S(2)}, u32[]{:S(2)}) async-start(bf16[32,64,1024]{2,1,0:T(8,128)(2,1)} %bitcast.122), calls=%async_computation.1 | async-start | bytes 8388608 | tf_op jit(solution)/shard_map/all_to_all | solution.py:22
  639.8 10.9 %all-to-all-start.3 = ((bf16[8,1,1]{2,1,0:T(2,128)(2,1)}), bf16[8,1,1]{2,1,0:T(2,128)(2,1)S(1)}, u32[]{:S(2)}, u32[]{:S(2)}) async-start(bf16[8,1,1]{2,1,0:T(2,128)(2,1)} %transpose_reshape.3), calls=%async_computation.4 | async-start | bytes 8192 | tf_op jit(solution)/shard_map/all_to_all | solution.py:22
  650.6 12.8 %all-to-all-start.1 = ((bf16[8,64,128]{2,1,0:T(8,128)(2,1)}), bf16[8,64,128]{2,1,0:T(8,128)(2,1)S(1)}, u32[]{:S(2)}, u32[]{:S(2)}) async-start(bf16[8,64,128]{2,1,0:T(8,128)(2,1)} %copy.31), calls=%async_computation.2 | async-start | bytes 262144 | tf_op jit(solution)/shard_map/all_to_all | solution.py:22
Sparse Core Ops, SparseCore 0:
  10.4 78.7 all-gather.3
  550.1 106.8 reduce-scatter.1
